TPU v7x, 32 devices: a whole 2x2x4 slice. The times are simulated.
32 devices in a mesh: mode: 8 (over z, y), cores: 4 (over x, core).
Axes of the slice: x: 2, y: 2, z: 4, core: 2. Of those that a mesh axis runs over, the one named last changes fastest.
Arguments:
- train_cores: bfloat16 [4, 400, 32, 400], P('cores', None, 'mode'), may hold values from -0.24748737 to 0.24748737
- sketch_cores: bfloat16 [4, 100, 32, 100], P('cores', None, 'mode'), may hold values from -0.3125 to 0.3125
- left_interface: float32 [100, 400], replicated, may hold values from -6 to 6
- right_sketch: bfloat16 [400, 100], replicated, may hold values from -6 to 6
Outputs:
- frames: bfloat16 [4, 100, 32, 100], P('cores', None, 'mode')
- interfaces: float32 [4, 100, 400], P('cores')
All inputs are finite; a program needn't handle non-finite values.
Results may differ from a plain program's by a relative error of at most 0.019.
Values may be sent and summed in bfloat16 or wider, within the bound.
A program may use at most 64 MiB of HBM per device.

v0:
```python
import math

import jax
import jax.numpy as jnp
from jax import lax
from jax.sharding import PartitionSpec as P


def from_behind(shard, axis, by):
    size = lax.axis_size(axis)
    pairs = [(i, i + by) for i in range(size) if 0 <= i + by < size]
    return lax.ppermute(shard, axis, pairs)


def body(train_cores, sketch_cores, left_interface, right_sketch):
    my_core = train_cores[0]
    my_sketch = sketch_cores[0]
    rank_size = my_core.shape[0]
    mode_local = my_core.shape[1]
    sketch_size = my_sketch.shape[0]
    group_index = lax.axis_index("cores")
    group_count = lax.axis_size("cores")
    final_group = group_count - 1
    flat_core = my_core.reshape(rank_size * mode_local, rank_size)
    sketch_flat = my_sketch.reshape(sketch_size, mode_local * sketch_size)
    sketch = right_sketch
    for round_index in range(group_count - 1):
        partial_value = jnp.dot(flat_core, sketch, preferred_element_type=jnp.float32).astype(
            jnp.bfloat16
        )
        partial_value = partial_value.reshape(rank_size, mode_local * sketch_size)
        local_term = lax.dot_general(
            partial_value, sketch_flat, (((1,), (1,)), ((), ())), preferred_element_type=jnp.float32
        )
        summed = lax.psum(local_term, "mode")
        received = from_behind(summed.astype(jnp.bfloat16), "cores", -1)
        sketch = jnp.where(group_index == final_group, right_sketch, received)
    frame_scale = math.sqrt(sketch_size * mode_local * lax.axis_size("mode"))
    wide_core = my_core.reshape(rank_size, mode_local * rank_size)
    interface = left_interface
    for round_index in range(group_count):
        carry_low = interface.astype(jnp.bfloat16)
        built = jnp.dot(carry_low, wide_core, preferred_element_type=jnp.float32)
        built = built.astype(jnp.bfloat16).reshape(sketch_size * mode_local, rank_size)
        images = jnp.dot(built, sketch, preferred_element_type=jnp.float32)
        core_local = lax.dot_general(
            built, built, (((0,), (0,)), ((), ())), preferred_element_type=jnp.float32
        )
        core_square = lax.psum(core_local, "mode")
        sketch_wide = sketch.astype(jnp.float32)
        projected = lax.dot_general(
            sketch_wide, core_square, (((0,), (0,)), ((), ())), precision=lax.Precision.HIGHEST
        )
        gram_matrix = jnp.dot(projected, sketch_wide, precision=lax.Precision.HIGHEST)
        chol_lower = jnp.linalg.cholesky(gram_matrix)
        frame_rows = lax.linalg.triangular_solve(chol_lower, images.T, left_side=True, lower=True)
        next_interface = lax.linalg.triangular_solve(
            chol_lower, projected, left_side=True, lower=True
        )
        frame_out = (frame_rows.T * frame_scale).astype(jnp.bfloat16)
        interface_out = next_interface
        if round_index < group_count - 1:
            passed = from_behind(next_interface.astype(jnp.bfloat16), "cores", 1)
            interface = jnp.where(group_index == 0, left_interface, passed.astype(jnp.float32))
    frames = frame_out.reshape(1, sketch_size, mode_local, sketch_size)
    interfaces = interface_out.reshape(1, sketch_size, rank_size)
    return (frames, interfaces)


def solution(mesh):
    in_specs = (P("cores", None, "mode", None), P("cores", None, "mode", None), P(), P())
    out_specs = (P("cores", None, "mode", None), P("cores", None, None))
    return jax.shard_map(body, mesh=mesh, in_specs=in_specs, out_specs=out_specs, check_vma=False)
```

profile of v0, /device:TPU:3, one launch (start us, length us, event | category | flops | bytes accessed | tf_op | source)
XLA Modules:
  0.0 526.4 jit_solution(15847679337264826134)
XLA Ops:
  7.2 2.8 reshape_squeeze.9
  11.7 33.2 %all-reduce.15 = bf16[400,100]{1,0:T(8,128)(2,1)} all-reduce(f32[400,100]{1,0:T(8,128)S(1)} %fusion.30), channel_id=1, replica_groups=mesh['mode'=8,'cores'=4] {'mode'}, use_global_device_ids=true, to_apply=%region_0.0 | all-reduce | flops 40000 | bytes 240000 | tf_op jit(solution)/shard_map/psum | solution.py:35
  44.9 10.6 %collective-permute-start = (bf16[400,100]{1,0:T(8,128)(2,1)}, bf16[400,100]{1,0:T(8,128)(2,1)}, u32[]{:S(2)}, u32[]{:S(2)}) collective-permute-start(bf16[400,100]{1,0:T(8,128)(2,1)} %all-reduce.15), channel_id=1, source_target_pairs={{1,0},{2,1},{3,2},{5,4},{6,5},{7,6},{9,8},{10,9},{11,10},{13,12},{... | collective-permute-start | bytes 240008 | tf_op jit(solution)/shard_map/ppermute | solution.py:12
  55.5 3.4 reshape_squeeze.11
  68.9 29.4 %all-reduce.16 = bf16[400,100]{1,0:T(8,128)(2,1)} all-reduce(f32[400,100]{1,0:T(8,128)} %fusion.31), channel_id=1, replica_groups=mesh['mode'=8,'cores'=4] {'mode'}, use_global_device_ids=true, to_apply=%region_1.2 | all-reduce | flops 40000 | bytes 240000 | tf_op jit(solution)/shard_map/psum | solution.py:35
  98.3 10.0 %collective-permute-start.1 = (bf16[400,100]{1,0:T(8,128)(2,1)}, bf16[400,100]{1,0:T(8,128)(2,1)}, u32[]{:S(2)}, u32[]{:S(2)}) collective-permute-start(bf16[400,100]{1,0:T(8,128)(2,1)} %all-reduce.16), channel_id=1, source_target_pairs={{1,0},{2,1},{3,2},{5,4},{6,5},{7,6},{9,8},{10,9},{11,10},{13,12},{... | collective-permute-start | bytes 240008 | tf_op jit(solution)/shard_map/ppermute | solution.py:12
  111.5 32.6 %all-reduce.17 = bf16[400,100]{1,0:T(8,128)(2,1)S(1)} all-reduce(f32[400,100]{1,0:T(8,128)S(1)} %fusion.32), channel_id=1, replica_groups=mesh['mode'=8,'cores'=4] {'mode'}, use_global_device_ids=true, to_apply=%region_2.3 | all-reduce | flops 40000 | bytes 240000 | tf_op jit(solution)/shard_map/psum | solution.py:35
  144.1 9.5 %collective-permute-start.2 = (bf16[400,100]{1,0:T(8,128)(2,1)S(1)}, bf16[400,100]{1,0:T(8,128)(2,1)S(1)}, u32[]{:S(2)}, u32[]{:S(2)}) collective-permute-start(bf16[400,100]{1,0:T(8,128)(2,1)S(1)} %all-reduce.17), channel_id=1, source_target_pairs={{1,0},{2,1},{3,2},{5,4},{6,5},{7,6},{9,8},{10,9},{11,10},{13,12},{... | collective-permute-start | bytes 240008 | tf_op jit(solution)/shard_map/ppermute | solution.py:12
  154.4 29.2 %all-reduce.8.cloned.1.call-done = f32[400,400]{1,0:T(8,128)} async-done(((f32[400,400]{1,0:T(8,128)}), f32[400,400]{1,0:T(8,128)}) %all-reduce.8.cloned.1.call-update) | async-done | bytes 640016 | tf_op jit(solution)/shard_map/psum | solution.py:49
  186.3 9.1 %cholesky.74 = f32[100,100]{1,0:T(8,128)S(1)} custom-call(f32[100,100]{1,0:T(8,128)S(1)} %fusion.23), custom_call_target="Cholesky" | custom-call | tf_op jit(solution)/shard_map/jit(cholesky)/cholesky | solution.py:55
  196.8 7.7 %custom-call.9 = f32[1,100,100]{1,2,0:T(8,128)S(1)} custom-call(f32[1,100,100]{2,1,0:T(8,128)S(1)} %fusion.11), custom_call_target="InvertDiagBlocksLowerTriangular" | custom-call | tf_op jit(solution)/shard_map/triangular_solve/custom-call.0 | solution.py:57
  206.1 3.8 collective-permute-done.3
  212.2 75.8 %all-reduce.10.cloned.1.call-done = f32[400,400]{1,0:T(8,128)} async-done(((f32[400,400]{1,0:T(8,128)}), f32[400,400]{1,0:T(8,128)}) %all-reduce.10.cloned.1.call-update) | async-done | bytes 640016 | tf_op jit(solution)/shard_map/psum | solution.py:49
  290.7 9.1 %cholesky.85 = f32[100,100]{1,0:T(8,128)S(1)} custom-call(f32[100,100]{1,0:T(8,128)S(1)} %fusion.21), custom_call_target="Cholesky" | custom-call | tf_op jit(solution)/shard_map/jit(cholesky)/cholesky | solution.py:55
  301.1 7.7 %custom-call.10 = f32[1,100,100]{1,2,0:T(8,128)S(1)} custom-call(f32[1,100,100]{2,1,0:T(8,128)S(1)} %fusion.12), custom_call_target="InvertDiagBlocksLowerTriangular" | custom-call | tf_op jit(solution)/shard_map/triangular_solve/custom-call.0 | solution.py:57
  310.7 3.8 collective-permute-done.4
  316.8 75.6 %all-reduce.12.cloned.1.call-done = f32[400,400]{1,0:T(8,128)} async-done(((f32[400,400]{1,0:T(8,128)}), f32[400,400]{1,0:T(8,128)}) %all-reduce.12.cloned.1.call-update) | async-done | bytes 640016 | tf_op jit(solution)/shard_map/psum | solution.py:49
  395.0 9.1 %cholesky.96 = f32[100,100]{1,0:T(8,128)S(1)} custom-call(f32[100,100]{1,0:T(8,128)S(1)} %fusion.19), custom_call_target="Cholesky" | custom-call | tf_op jit(solution)/shard_map/jit(cholesky)/cholesky | solution.py:55
  405.5 7.7 %custom-call.11 = f32[1,100,100]{1,2,0:T(8,128)S(1)} custom-call(f32[1,100,100]{2,1,0:T(8,128)S(1)} %fusion.13), custom_call_target="InvertDiagBlocksLowerTriangular" | custom-call | tf_op jit(solution)/shard_map/triangular_solve/custom-call.0 | solution.py:57
  415.0 3.6 collective-permute-done.5
  421.1 75.6 %all-reduce.14.cloned.1.call-done = f32[400,400]{1,0:T(8,128)} async-done(((f32[400,400]{1,0:T(8,128)}), f32[400,400]{1,0:T(8,128)}) %all-reduce.14.cloned.1.call-update) | async-done | bytes 640016 | tf_op jit(solution)/shard_map/psum | solution.py:49
  496.7 2.1 fusion.43
  499.3 9.1 %cholesky.107 = f32[100,100]{1,0:T(8,128)S(1)} custom-call(f32[100,100]{1,0:T(8,128)S(1)} %fusion.17), custom_call_target="Cholesky" | custom-call | tf_op jit(solution)/shard_map/jit(cholesky)/cholesky | solution.py:55
  509.8 7.7 %custom-call.12 = f32[1,100,100]{1,2,0:T(8,128)S(1)} custom-call(f32[1,100,100]{2,1,0:T(8,128)S(1)} %fusion.14), custom_call_target="InvertDiagBlocksLowerTriangular" | custom-call | tf_op jit(solution)/shard_map/triangular_solve/custom-call.0 | solution.py:56
  (88 shorter events, 43.8 us)
Async XLA Ops:
  7.2 2.9 copy-start.4
  7.2 176.5 %all-reduce.8.cloned.1.call-start = ((), (), s32[]{:S(2)}) async-start(), calls=%async_computation | async-start | bytes 1638400 | tf_op jit(solution)/shard_map/psum | solution.py:49
  10.1 1.2 copy-start.6
  11.4 33.5 %copy-start.2 = (bf16[100,400]{1,0:T(8,128)(2,1)}, bf16[100,400]{1,0:T(8,128)(2,1)S(1)}, u32[]{:S(2)}) copy-start(bf16[100,400]{1,0:T(8,128)(2,1)S(1)} %reshape.69) | copy-start | bytes 240004
  44.9 14.0 %copy-start = (f32[100,400]{0,1:T(8,128)S(1)}, f32[100,400]{0,1:T(8,128)}, u32[]{:S(2)}) copy-start(f32[100,400]{0,1:T(8,128)} %param.9) | copy-start | bytes 480004
  44.9 16.6 %collective-permute-start = (bf16[400,100]{1,0:T(8,128)(2,1)}, bf16[400,100]{1,0:T(8,128)(2,1)}, u32[]{:S(2)}, u32[]{:S(2)}) collective-permute-start(bf16[400,100]{1,0:T(8,128)(2,1)} %all-reduce.15), channel_id=1, source_target_pairs={{1,0},{2,1},{3,2},{5,4},{6,5},{7,6},{9,8},{10,9},{11,10},{13,12},{... | collective-permute-start | bytes 240008 | tf_op jit(solution)/shard_map/ppermute | solution.py:12
  98.3 11.3 %collective-permute-start.1 = (bf16[400,100]{1,0:T(8,128)(2,1)}, bf16[400,100]{1,0:T(8,128)(2,1)}, u32[]{:S(2)}, u32[]{:S(2)}) collective-permute-start(bf16[400,100]{1,0:T(8,128)(2,1)} %all-reduce.16), channel_id=1, source_target_pairs={{1,0},{2,1},{3,2},{5,4},{6,5},{7,6},{9,8},{10,9},{11,10},{13,12},{... | collective-permute-start | bytes 240008 | tf_op jit(solution)/shard_map/ppermute | solution.py:12
  109.6 178.4 %all-reduce.10.cloned.1.call-start = ((), (), s32[]{:S(2)}) async-start(), calls=%async_computation.1 | async-start | bytes 1638400 | tf_op jit(solution)/shard_map/psum | solution.py:49
  110.3 0.9 copy-start.3
  110.3 44.1 %copy-start.5 = (bf16[400,100]{1,0:T(8,128)(2,1)S(1)}, bf16[400,100]{1,0:T(8,128)(2,1)}, u32[]{:S(2)}) copy-start(bf16[400,100]{1,0:T(8,128)(2,1)} %param.10) | copy-start | bytes 240004
  144.1 65.8 %copy-start.1 = (f32[100,400]{0,1:T(8,128)S(1)}, f32[100,400]{0,1:T(8,128)}, u32[]{:S(2)}) copy-start(f32[100,400]{0,1:T(8,128)} %param.9) | copy-start | bytes 480004
  144.1 10.3 %collective-permute-start.2 = (bf16[400,100]{1,0:T(8,128)(2,1)S(1)}, bf16[400,100]{1,0:T(8,128)(2,1)S(1)}, u32[]{:S(2)}, u32[]{:S(2)}) collective-permute-start(bf16[400,100]{1,0:T(8,128)(2,1)S(1)} %all-reduce.17), channel_id=1, source_target_pairs={{1,0},{2,1},{3,2},{5,4},{6,5},{7,6},{9,8},{10,9},{11,10},{13,12},{... | collective-permute-start | bytes 240008 | tf_op jit(solution)/shard_map/ppermute | solution.py:12
  204.8 5.1 collective-permute-start.3
  212.1 180.2 %all-reduce.12.cloned.1.call-start = ((), (), s32[]{:S(2)}) async-start(), calls=%async_computation.2 | async-start | bytes 1638400 | tf_op jit(solution)/shard_map/psum | solution.py:49
  309.1 5.3 %collective-permute-start.4 = (bf16[100,400]{0,1:T(8,128)(2,1)S(1)}, bf16[100,400]{0,1:T(8,128)(2,1)S(1)}, u32[]{:S(2)}, u32[]{:S(2)}) collective-permute-start(bf16[100,400]{0,1:T(8,128)(2,1)S(1)} %convolution_convert_fusion.8), channel_id=1, source_target_pairs={{0,1},{1,2},{2,3},{4,5},{5,6},{6,7},{8,9},{9,10},{10,11},{12,13},{... | collective-permute-start | bytes 240008 | tf_op jit(solution)/shard_map/ppermute | solution.py:12
  316.7 180.0 %all-reduce.14.cloned.1.call-start = ((), (), s32[]{:S(2)}) async-start(), calls=%async_computation.3 | async-start | bytes 1638400 | tf_op jit(solution)/shard_map/psum | solution.py:49
  413.5 5.1 collective-permute-start.5
Sparse Core Ops, SparseCore 0:
  109.7 73.9 all-reduce.7
  212.3 75.7 all-reduce.9
  316.8 75.4 all-reduce.11
  420.9 75.7 all-reduce.13
where the time goes:
time: 531 us; the launch traced here: 526 us
  waiting for transfers between devices  268 us (50%)
  blocking collectives  95.3 us (18%)
  other arithmetic  72.6 us (14%)
  starting transfers between devices  34.6 us (7%)
  matrix products  25.5 us (5%)
  local copies, waits for them, and re-layouts  16 us (3%)
  between operations  14.2 us (3%)
    psum x4, waiting for transfers between devices, body(): core_square = lax.psum(core_local, 'mode')  256 us
    psum x3, blocking collectives, body(): summed = lax.psum(local_term, 'mode')  95.3 us
    another operation x12, other arithmetic, body(): chol_lower = jnp.linalg.cholesky(gram_matrix)  39.3 us
    ppermute x6, starting transfers between devices, from_behind(): return lax.ppermute(shard, axis, pairs)  34.4 us
    another operation x6, other arithmetic, body(): lax.linalg.triangular_solve(chol_lower, projected, left_side=True, lower=...  25 us
    ppermute x6, waiting for transfers between devices, from_behind(): return lax.ppermute(shard, axis, pairs)  11.9 us
  transfers between devices with their start and end apart: 10, of which 8 were waited for; matrix products, arithmetic and copies ran while one was open for 2% of the time, Pallas kernels for 0%

commit v1 on v0

v1 whole, which is shorter than its diff:
```python
import functools
import math

import jax
import jax.numpy as jnp
from jax import lax
from jax.experimental import pallas as pl
from jax.experimental.pallas import tpu as pltpu
from jax.sharding import PartitionSpec as P

MESH = pl.DeviceIdType.MESH
F32, BF16 = jnp.float32, jnp.bfloat16
EXACT = lax.Precision.HIGHEST


def up(value, step):
    return -(-value // step) * step


def dot(a, b, ca, cb, precision=None):
    return lax.dot_general(
        a, b, (((ca,), (cb,)), ((), ())), preferred_element_type=F32, precision=precision
    )


def when(condition, run):
    if condition is True:
        run()
    else:
        pl.when(condition)(run)


def lower_inverse(gram, size, look=4):
    full = gram.shape[0]
    lane = lax.broadcasted_iota(jnp.int32, (1, full), 1)
    top, table, done = 0, gram, []
    for first in range(0, size, look):
        base = first // 8 * 8
        if base > top:
            done.append(table[: base - top])
            table = table[base - top :]
            top = base
        rows = full - top
        width = min(look, size - first)
        row_id = lax.broadcasted_iota(jnp.int32, (rows, full), 0) + top
        columns = [
            jnp.broadcast_to(table[:, first + t : first + t + 1], (rows, full)) for t in range(width)
        ]
        for t in range(width):
            j = first + t
            here = j - top
            column = columns[t]
            pivot = column[here : here + 1]
            inverse = 1.0 / pivot
            row = jnp.where(lane == j, 1.0, table[here : here + 1]) * inverse
            below = row_id > j
            lower = jnp.where(below, column, 0.0)
            for s in range(t + 1, width):
                ahead = here + s - t
                columns[s] = columns[s] - lower * (column[ahead : ahead + 1] * inverse)
            table = jnp.where((lane == j) & below, 0.0, table) - lower * row
    done.append(table)
    table = jnp.concatenate(done, axis=0) if len(done) > 1 else table
    row_id = lax.broadcasted_iota(jnp.int32, (full, full), 0)
    lane = lax.broadcasted_iota(jnp.int32, (full, full), 1)
    pivots = jnp.sum(jnp.where(row_id == lane, table, 0.0), axis=1, keepdims=True)
    unit = jnp.where(row_id > lane, table, jnp.where(row_id == lane, 1.0, 0.0))
    return unit * lax.rsqrt(pivots)


def kernel(
    dims,
    core_ref,
    gauss_ref,
    left_ref,
    right_ref,
    frames_ref,
    faces_ref,
    sketch_buf,
    part_out,
    part_in,
    carry_buf,
    carry_own,
    proj_out,
    proj_in,
    gram_out,
    gram_in,
    piece_sk,
    piece_ca,
    s_part,
    r_part,
    s_sk,
    r_sk,
    s_proj,
    r_proj,
    s_gram,
    r_gram,
    s_next,
    r_next,
    s_own,
    r_own,
):
    size, group_count, rank, sketch, modes, chunk, owners, scale = dims
    rank_pad, sketch_pad = owners * chunk, gauss_ref.shape[1]
    me = lax.axis_index("mode")
    group = lax.axis_index("cores")
    final = group_count - 1
    owner = True if owners == size else me < owners

    def scatter(out_ref, in_ref, sends, recvs, target=None):
        copies = []
        for d in range(1, size):
            peer = lax.rem(me + d, size)
            copies.append(
                pltpu.make_async_remote_copy(
                    src_ref=out_ref.at[peer] if target is None else out_ref,
                    dst_ref=in_ref.at[d],
                    send_sem=sends.at[d],
                    recv_sem=recvs.at[d],
                    device_id={"mode": peer},
                    device_id_type=MESH,
                )
            )
        return copies

    def chunk_sends(copies, act):
        for d, copy in enumerate(copies, 1):
            peer = lax.rem(me + d, size)
            when(True if owners == size else peer < owners, functools.partial(act, copy))

    def spread(piece_ref, buf_ref, sends, recvs, to_group, skip_self):
        copies = []
        for d in range(1 if skip_self else 0, size):
            peer = lax.rem(me + d, size)
            copies.append(
                pltpu.make_async_remote_copy(
                    src_ref=piece_ref,
                    dst_ref=buf_ref.at[me],
                    send_sem=sends.at[d],
                    recv_sem=recvs.at[me],
                    device_id={"mode": peer, "cores": to_group},
                    device_id_type=MESH,
                )
            )
        return copies

    def await_chunk(buf_ref, recvs, source):
        pltpu.make_async_remote_copy(
            src_ref=buf_ref.at[source],
            dst_ref=buf_ref.at[source],
            send_sem=recvs.at[source],
            recv_sem=recvs.at[source],
            device_id={"mode": lax.rem(me + 1, size)},
            device_id_type=MESH,
        ).wait_recv()

    @pl.when(group == final)
    def _():
        sketch_buf[...] = right_ref[...].reshape(sketch_buf.shape)

    @pl.when(group < final)
    def _():
        for source in range(owners):
            await_chunk(sketch_buf, r_sk, source)

    down = lax.rem(group + group_count - 1, group_count)
    upward = lax.rem(group + 1, group_count)
    part_copies = scatter(part_out, part_in, s_part, r_part)
    sk_copies = spread(piece_sk, sketch_buf, s_sk, r_sk, down, False)

    @pl.when(group > 0)
    def _():
        held = sketch_buf[...].reshape(rank_pad, sketch_pad)
        total = None
        for i in range(modes):
            partial_value = dot(core_ref[i], held, 1, 0).astype(BF16)
            term = dot(partial_value, gauss_ref[i], 1, 1)
            total = term if total is None else total + term
        part_out[...] = total.astype(part_out.dtype).reshape(part_out.shape)
        chunk_sends(part_copies, lambda c: c.start())

        def finish():
            value = part_out[me].astype(F32)
            for d in range(1, size):
                part_copies[d - 1].wait_recv()
                value = value + part_in[d].astype(F32)
            piece_sk[...] = value.astype(BF16)
            for copy in sk_copies:
                copy.start()
            for copy in sk_copies:
                copy.wait_send()

        when(owner, finish)
        chunk_sends(part_copies, lambda c: c.wait_send())

    @pl.when(group == 0)
    def _():
        carry_buf[...] = left_ref[...].reshape(carry_buf.shape)

    @pl.when(group > 0)
    def _():
        for source in range(owners):
            await_chunk(carry_buf, r_next, source)

    carry = carry_buf[...].reshape(rank_pad, sketch_pad)
    held = sketch_buf[...].reshape(rank_pad, sketch_pad)
    gram_copies = scatter(gram_out, gram_in, s_gram, r_gram, True)
    proj_copies = scatter(proj_out, proj_in, s_proj, r_proj)
    images, halves, builts = [], [], []
    gram = None
    for i in range(modes):
        built = dot(carry, core_ref[i], 0, 0).astype(BF16)
        image = dot(built, held, 1, 0)
        high = image.astype(BF16)
        low = (image - high.astype(F32)).astype(BF16)
        cross = dot(high, low, 0, 0)
        term = dot(high, high, 0, 0) + dot(low, high, 0, 0) + cross
        gram = term if gram is None else gram + term
        images.append(image)
        halves.append((high, low))
        builts.append(built)
    gram_rows = gram_out.shape[0]
    gram_out[...] = gram[:gram_rows]
    for copy in gram_copies:
        copy.start()
    proj = None
    for (high, low), built in zip(halves, builts):
        term = dot(built, high, 0, 0) + dot(built, low, 0, 0)
        proj = term if proj is None else proj + term
    proj_out[...] = proj.astype(proj_out.dtype).reshape(proj_out.shape)
    chunk_sends(proj_copies, lambda c: c.start())

    for copy in gram_copies:
        copy.wait_recv()
    gram_in[0] = gram_out[...]
    total = None
    for source in range(size):
        term = gram_in[lax.rem(me - source + size, size)]
        total = term if total is None else total + term
    if gram_rows < sketch_pad:
        total = jnp.concatenate([total, jnp.zeros((sketch_pad - gram_rows, sketch_pad), F32)], 0)
    row_id = lax.broadcasted_iota(jnp.int32, (sketch_pad, sketch_pad), 0)
    lane_id = lax.broadcasted_iota(jnp.int32, (sketch_pad, sketch_pad), 1)
    total = jnp.where((row_id == lane_id) & (row_id >= sketch), 1.0, total)
    inverse = lower_inverse(total, sketch)

    next_copies = spread(piece_ca, carry_buf, s_next, r_next, upward, False)
    own_copies = spread(piece_ca, carry_own, s_own, r_own, group, True)

    def project():
        value = proj_out[me].astype(F32)
        for d in range(1, size):
            proj_copies[d - 1].wait_recv()
            value = value + proj_in[d].astype(F32)
        piece_ca[...] = dot(value, inverse, 1, 1, EXACT).astype(BF16)

        @pl.when(group < final)
        def _():
            for copy in next_copies:
                copy.start()

        for copy in own_copies:
            copy.start()
        carry_own[me] = piece_ca[...]

    when(owner, project)
    for i in range(modes):
        orth = dot(images[i], inverse, 1, 1, EXACT)
        frames_ref[i] = (orth * scale).astype(BF16)
    chunk_sends(proj_copies, lambda c: c.wait_send())
    for copy in gram_copies:
        copy.wait_send()
    for source in range(owners):

        @pl.when(me != source)
        def _(source=source):
            await_chunk(carry_own, r_own, source)

    faces = carry_own[...].reshape(rank_pad, sketch_pad).astype(F32).T
    faces_ref[...] = faces

    def drain():
        for copy in own_copies:
            copy.wait_send()

        @pl.when(group < final)
        def _():
            for copy in next_copies:
                copy.wait_send()

    when(owner, drain)


def body(train_cores, sketch_cores, left_interface, right_sketch):
    size = lax.axis_size("mode")
    group_count = lax.axis_size("cores")
    _, rank, modes, _ = train_cores.shape
    sketch = sketch_cores.shape[1]
    sketch_pad = up(sketch, 128)
    chunk = up(-(-up(rank, 128) // size), 16)
    owners = -(-rank // chunk)
    chunk_total = owners * chunk
    rank_pad = up(chunk_total, 128)
    owners = rank_pad // chunk if rank_pad % chunk == 0 else owners
    rank_pad = owners * chunk
    core = jnp.pad(
        train_cores[0].transpose(1, 0, 2), ((0, 0), (0, rank_pad - rank), (0, rank_pad - rank))
    )
    gauss = jnp.pad(
        sketch_cores[0].transpose(1, 0, 2),
        ((0, 0), (0, sketch_pad - sketch), (0, sketch_pad - sketch)),
    )
    left = jnp.pad(
        left_interface.astype(BF16).T, ((0, rank_pad - rank), (0, sketch_pad - sketch))
    )
    right = jnp.pad(right_sketch, ((0, rank_pad - rank), (0, sketch_pad - sketch)))
    scale = math.sqrt(sketch * modes * size)
    dims = (size, group_count, rank, sketch, modes, chunk, owners, scale)
    gram_rows = up(sketch, 8)
    chunks = (owners, chunk, sketch_pad)
    vmem = pl.BlockSpec(memory_space=pltpu.VMEM)
    dma = pltpu.SemaphoreType.DMA((size,))
    frames, faces = pl.pallas_call(
        functools.partial(kernel, dims),
        out_shape=(
            jax.ShapeDtypeStruct((modes, sketch_pad, sketch_pad), BF16),
            jax.ShapeDtypeStruct((sketch_pad, rank_pad), F32),
        ),
        in_specs=[vmem] * 4,
        out_specs=(vmem, vmem),
        scratch_shapes=[
            pltpu.VMEM(chunks, BF16),
            pltpu.VMEM(chunks, F32),
            pltpu.VMEM((size, chunk, sketch_pad), F32),
            pltpu.VMEM(chunks, BF16),
            pltpu.VMEM(chunks, BF16),
            pltpu.VMEM(chunks, F32),
            pltpu.VMEM((size, chunk, sketch_pad), F32),
            pltpu.VMEM((gram_rows, sketch_pad), F32),
            pltpu.VMEM((size, gram_rows, sketch_pad), F32),
            pltpu.VMEM((chunk, sketch_pad), BF16),
            pltpu.VMEM((chunk, sketch_pad), BF16),
        ]
        + [dma] * 12,
        compiler_params=pltpu.CompilerParams(has_side_effects=True),
    )(core, gauss, left, right)
    frames = frames[:, :sketch, :sketch].transpose(1, 0, 2)[None]
    return frames, faces[None, :sketch, :rank]


def solution(mesh):
    in_specs = (P("cores", None, "mode", None), P("cores", None, "mode", None), P(), P())
    out_specs = (P("cores", None, "mode", None), P("cores", None, None))
    return jax.shard_map(body, mesh=mesh, in_specs=in_specs, out_specs=out_specs, check_vma=False)
```

time: 531 us -> 122 us (0.23)
  waiting for transfers between devices: 268 us -> 0 us
  Pallas kernels: 0 us -> 112 us
  blocking collectives: 95.3 us -> 0 us
  other arithmetic: 72.6 us -> 0.01 us
  starting transfers between devices: 34.6 us -> 0 us
  matrix products: 25.5 us -> 0 us
  between operations: 14.2 us -> 0.68 us
  local copies, waits for them, and re-layouts: 16 us -> 8.81 us
    psum x4 -> x0, waiting for transfers between devices: 256 us -> none  [body(): core_square = lax.psum(core_local, 'mode')]
    pallas_call x0 -> x1, Pallas kernels: none -> 112 us  [body(): pl.pallas_call(functools.partial(kernel, dims), out_shape=(jax.ShapeDtype...]
    psum x3 -> x0, blocking collectives: 95.3 us -> none  [body(): summed = lax.psum(local_term, 'mode')]
    another operation x20 -> x0, other arithmetic: 72.6 us -> none  [the longest x12 39.3 us: body(): chol_lower = jnp.linalg.cholesky(gram_matrix)]
    ppermute x6 -> x0, starting transfers between devices: 34.4 us -> none  [from_behind(): return lax.ppermute(shard, axis, pairs)]
    dot_general x23 -> x0, matrix products: 23 us -> none  [the longest x4 8.36 us: body(): lax.dot_general(sketch_wide, core_square, (((0,), (0,)), ((), ())), preci...]
    ppermute x6 -> x0, waiting for transfers between devices: 11.9 us -> none  [from_behind(): return lax.ppermute(shard, axis, pairs)]
    another operation x3 -> x0, local copies, waits for them, and re-layouts: 6.37 us -> none  [the longest x1 3.41 us: body(): wide_core = my_core.reshape(rank_size, mode_local * rank_size)]
  transfers between devices with their start and end apart: 10 -> 0, of which waited for: 8 -> 0; matrix products, arithmetic and copies ran while one was open for 2% -> 0% of each run, Pallas kernels for 0% -> 0%
where the time goes in v1:
time: 122 us
  Pallas kernels  112 us (92%)
  local copies, waits for them, and re-layouts  8.81 us (7%)
    pallas_call x1, Pallas kernels, body(): pl.pallas_call(functools.partial(kernel, dims), out_shape=(jax.ShapeDtype...  112 us
    unnamed x10, local copies, waits for them, and re-layouts  3.35 us

profile of v1, /device:TPU:3, one launch (start us, length us, event | category | flops | bytes accessed | tf_op | source)
XLA Modules:
  0.0 121.7 jit_solution(4753639471440218636)
XLA Ops:
  0.6 1.7 %copy.12 = bf16[1,400,4,400]{3,1,2,0:T(8,128)(2,1)S(1)} copy(bf16[1,400,4,400]{3,2,1,0:T(4,128)(2,1)} %param.4) | data formatting | bytes 2560000 | tf_op args[0]
  2.4 0.0 copy-start.2
  2.4 0.0 copy-start
  2.4 0.0 copy-start.1
  2.4 1.6 %pad.15.core_ref = bf16[4,512,512]{2,1,0:T(8,128)(2,1)} pad(bf16[4,400,400]{2,1,0:T(8,128)(2,1)S(1)} %bitcast.18, bf16[]{:T(256)} %constant.2.clone.1), padding=0_0x0_112x0_112 | pad | bytes 3377154 | tf_op jit(solution)/shard_map/jit(_pad)/pad | solution.py:306
  4.0 0.0 copy-done.2
  4.0 0.7 pad.16.gauss_ref
  4.7 0.0 copy-done
  4.7 0.7 pad.17.left_ref
  5.4 0.0 copy-done.1
  5.4 0.7 pad.18.right_ref
  6.1 112.1 %shard_map.59 = (bf16[4,128,128]{2,1,0:T(8,128)(2,1)}, f32[128,512]{1,0:T(8,128)}) custom-call(bf16[4,512,512]{2,1,0:T(8,128)(2,1)} %pad.15.core_ref, bf16[4,128,128]{2,1,0:T(8,128)(2,1)} %pad.16.gauss_ref, bf16[512,128]{1,0:T(8,128)(2,1)} %pad.17.left_ref, bf16[512,128]{1,0:T(8,128)(2,1)} %pad.18.right_ref), custom_call_target="tpu_custom_call" | custom-call | tf_op jit(solution)/shard_map/pallas_call | solution.py:323
  118.2 0.9 slice_bitcast_fusion
  119.2 0.9 copy.9
  120.1 0.9 slice_bitcast_fusion.1
  121.0 0.7 copy.8
  (2 shorter events, 0.0 us)
Async XLA Ops:
  2.4 1.6 %copy-start.2 = (bf16[1,100,4,100]{3,2,1,0:T(4,128)(2,1)S(1)}, bf16[1,100,4,100]{3,2,1,0:T(4,128)(2,1)}, u32[]{:S(2)}) copy-start(bf16[1,100,4,100]{3,2,1,0:T(4,128)(2,1)} %param.5) | copy-start | bytes 240004
  2.4 2.3 %copy-start = (f32[100,400]{0,1:T(8,128)S(1)}, f32[100,400]{0,1:T(8,128)}, u32[]{:S(2)}) copy-start(f32[100,400]{0,1:T(8,128)} %param.6) | copy-start | bytes 480004
  2.4 3.0 %copy-start.1 = (bf16[400,100]{1,0:T(8,128)(2,1)S(1)}, bf16[400,100]{1,0:T(8,128)(2,1)}, u32[]{:S(2)}) copy-start(bf16[400,100]{1,0:T(8,128)(2,1)} %param.7) | copy-start | bytes 240004

commit v2 on v1

--- a/solution.py
+++ b/solution.py
@@ -101,19 +101,47 @@
     r_own,
 ):
     size, group_count, rank, sketch, modes, chunk, owners, scale = dims
-    rank_pad, sketch_pad = owners * chunk, gauss_ref.shape[1]
+    rank_pad, sketch_pad = sketch_buf.shape
     me = lax.axis_index("mode")
     group = lax.axis_index("cores")
     final = group_count - 1
     owner = True if owners == size else me < owners
-
-    def scatter(out_ref, in_ref, sends, recvs, target=None):
+    down = lax.rem(group + group_count - 1, group_count)
+    upward = lax.rem(group + 1, group_count)
+
+    barrier = pltpu.get_barrier_semaphore()
+
+    def greet(to_group, first):
+        for d in range(first, size):
+            pl.semaphore_signal(
+                barrier,
+                inc=1,
+                device_id={"mode": lax.rem(me + d, size), "cores": to_group},
+                device_id_type=MESH,
+            )
+
+    greet(group, 1)
+    pl.when(group < final)(lambda: greet(upward, 0))
+    pl.when(group > 0)(lambda: greet(down, 0))
+
+    @pl.when(group == 0)
+    def _():
+        pl.semaphore_wait(barrier, 2 * size - 1)
+
+    @pl.when((group > 0) & (group < final))
+    def _():
+        pl.semaphore_wait(barrier, 3 * size - 1)
+
+    def block(ref, index):
+        return ref.at[pl.ds(pl.multiple_of(index * chunk, chunk), chunk)]
+
+    def scatter(out_ref, in_ref, sends, recvs, whole=False):
         copies = []
         for d in range(1, size):
             peer = lax.rem(me + d, size)
             copies.append(
                 pltpu.make_async_remote_copy(
-                    src_ref=out_ref.at[peer] if target is None else out_ref,
+                    src_ref=out_ref if whole else block(out_ref, peer),
                     dst_ref=in_ref.at[d],
                     send_sem=sends.at[d],
                     recv_sem=recvs.at[d],
@@ -128,14 +156,14 @@
             peer = lax.rem(me + d, size)
             when(True if owners == size else peer < owners, functools.partial(act, copy))
 
-    def spread(piece_ref, buf_ref, sends, recvs, to_group, skip_self):
+    def spread(piece_ref, buf_ref, sends, recvs, to_group, first):
         copies = []
-        for d in range(1 if skip_self else 0, size):
+        for d in range(first, size):
             peer = lax.rem(me + d, size)
             copies.append(
                 pltpu.make_async_remote_copy(
                     src_ref=piece_ref,
-                    dst_ref=buf_ref.at[me],
+                    dst_ref=block(buf_ref, me),
                     send_sem=sends.at[d],
                     recv_sem=recvs.at[me],
                     device_id={"mode": peer, "cores": to_group},
@@ -146,41 +174,49 @@
 
     def await_chunk(buf_ref, recvs, source):
         pltpu.make_async_remote_copy(
-            src_ref=buf_ref.at[source],
-            dst_ref=buf_ref.at[source],
+            src_ref=block(buf_ref, source),
+            dst_ref=block(buf_ref, source),
             send_sem=recvs.at[source],
             recv_sem=recvs.at[source],
             device_id={"mode": lax.rem(me + 1, size)},
             device_id_type=MESH,
         ).wait_recv()
 
+    if rank_pad > rank:
+        rest = jnp.zeros((rank_pad - rank, sketch_pad), F32)
+        part_out[pl.ds(rank, rank_pad - rank), :] = rest.astype(part_out.dtype)
+        proj_out[pl.ds(rank, rank_pad - rank), :] = rest
+
     @pl.when(group == final)
     def _():
-        sketch_buf[...] = right_ref[...].reshape(sketch_buf.shape)
+        sketch_buf[...] = right_ref[...]
 
     @pl.when(group < final)
     def _():
         for source in range(owners):
             await_chunk(sketch_buf, r_sk, source)
 
-    down = lax.rem(group + group_count - 1, group_count)
-    upward = lax.rem(group + 1, group_count)
     part_copies = scatter(part_out, part_in, s_part, r_part)
-    sk_copies = spread(piece_sk, sketch_buf, s_sk, r_sk, down, False)
+    sk_copies = spread(piece_sk, sketch_buf, s_sk, r_sk, down, 0)
+    held = sketch_buf[pl.ds(0, rank), :]
+    partials = [dot(core_ref[i], held, 1, 0).astype(BF16) for i in range(modes)]
 
     @pl.when(group > 0)
     def _():
-        held = sketch_buf[...].reshape(rank_pad, sketch_pad)
         total = None
         for i in range(modes):
-            partial_value = dot(core_ref[i], held, 1, 0).astype(BF16)
-            term = dot(partial_value, gauss_ref[i], 1, 1)
+            term = dot(partials[i], gauss_ref[i], 1, 1)
             total = term if total is None else total + term
-        part_out[...] = total.astype(part_out.dtype).reshape(part_out.shape)
+        part_out[pl.ds(0, rank), :] = total.astype(part_out.dtype)
+
+        @pl.when(group == final)
+        def _():
+            pl.semaphore_wait(barrier, 2 * size - 1)
+
         chunk_sends(part_copies, lambda c: c.start())
 
         def finish():
-            value = part_out[me].astype(F32)
+            value = block(part_out, me)[...].astype(F32)
             for d in range(1, size):
                 part_copies[d - 1].wait_recv()
                 value = value + part_in[d].astype(F32)
@@ -195,44 +231,38 @@
 
     @pl.when(group == 0)
     def _():
-        carry_buf[...] = left_ref[...].reshape(carry_buf.shape)
+        carry_buf[...] = left_ref[...]
 
     @pl.when(group > 0)
     def _():
         for source in range(owners):
             await_chunk(carry_buf, r_next, source)
 
-    carry = carry_buf[...].reshape(rank_pad, sketch_pad)
-    held = sketch_buf[...].reshape(rank_pad, sketch_pad)
+    carry = carry_buf[pl.ds(0, rank), :].T
     gram_copies = scatter(gram_out, gram_in, s_gram, r_gram, True)
     proj_copies = scatter(proj_out, proj_in, s_proj, r_proj)
-    images, halves, builts = [], [], []
-    gram = None
-    for i in range(modes):
-        built = dot(carry, core_ref[i], 0, 0).astype(BF16)
-        image = dot(built, held, 1, 0)
-        high = image.astype(BF16)
-        low = (image - high.astype(F32)).astype(BF16)
-        cross = dot(high, low, 0, 0)
-        term = dot(high, high, 0, 0) + dot(low, high, 0, 0) + cross
-        gram = term if gram is None else gram + term
-        images.append(image)
-        halves.append((high, low))
-        builts.append(built)
+    images = [dot(carry, partials[i], 1, 0) for i in range(modes)]
+    image = jnp.concatenate(images, axis=0)
+    high = image.astype(BF16)
+    low = (image - high.astype(F32)).astype(BF16)
+    pair = jnp.concatenate([high, low], axis=1)
+    terms = dot(high, pair, 0, 0)
+    cross = terms[:, sketch_pad:]
+    gram = terms[:, :sketch_pad] + cross + cross.T
     gram_rows = gram_out.shape[0]
     gram_out[...] = gram[:gram_rows]
     for copy in gram_copies:
         copy.start()
-    proj = None
-    for (high, low), built in zip(halves, builts):
-        term = dot(built, high, 0, 0) + dot(built, low, 0, 0)
-        proj = term if proj is None else proj + term
-    proj_out[...] = proj.astype(proj_out.dtype).reshape(proj_out.shape)
+    built = jnp.concatenate(
+        [dot(carry, core_ref[i], 1, 0).astype(BF16) for i in range(modes)], axis=0
+    )
+    proj = dot(built, pair, 0, 0)
+    proj_out[pl.ds(0, rank), :] = proj[:, :sketch_pad] + proj[:, sketch_pad:]
     chunk_sends(proj_copies, lambda c: c.start())
 
+    gram_in[0] = gram_out[...]
     for copy in gram_copies:
         copy.wait_recv()
-    gram_in[0] = gram_out[...]
     total = None
     for source in range(size):
         term = gram_in[lax.rem(me - source + size, size)]
@@ -242,16 +272,16 @@
     row_id = lax.broadcasted_iota(jnp.int32, (sketch_pad, sketch_pad), 0)
     lane_id = lax.broadcasted_iota(jnp.int32, (sketch_pad, sketch_pad), 1)
     total = jnp.where((row_id == lane_id) & (row_id >= sketch), 1.0, total)
-    inverse = lower_inverse(total, sketch)
-
-    next_copies = spread(piece_ca, carry_buf, s_next, r_next, upward, False)
-    own_copies = spread(piece_ca, carry_own, s_own, r_own, group, True)
+    inverse = lower_inverse(total, sketch, 8)
+
+    next_copies = spread(piece_ca, carry_buf, s_next, r_next, upward, 0)
+    own_copies = spread(piece_ca, carry_own, s_own, r_own, group, 1)
 
     def project():
-        value = proj_out[me].astype(F32)
+        value = block(proj_out, me)[...]
         for d in range(1, size):
             proj_copies[d - 1].wait_recv()
-            value = value + proj_in[d].astype(F32)
+            value = value + proj_in[d]
         piece_ca[...] = dot(value, inverse, 1, 1, EXACT).astype(BF16)
 
         @pl.when(group < final)
@@ -261,12 +291,12 @@
 
         for copy in own_copies:
             copy.start()
-        carry_own[me] = piece_ca[...]
+        block(carry_own, me)[...] = piece_ca[...]
 
     when(owner, project)
+    orth = (dot(image, inverse, 1, 1, EXACT) * scale).astype(BF16)
     for i in range(modes):
-        orth = dot(images[i], inverse, 1, 1, EXACT)
-        frames_ref[i] = (orth * scale).astype(BF16)
+        frames_ref[i] = orth[i * sketch_pad : (i + 1) * sketch_pad]
     chunk_sends(proj_copies, lambda c: c.wait_send())
     for copy in gram_copies:
         copy.wait_send()
@@ -276,8 +306,7 @@
         def _(source=source):
             await_chunk(carry_own, r_own, source)
 
-    faces = carry_own[...].reshape(rank_pad, sketch_pad).astype(F32).T
-    faces_ref[...] = faces
+    faces_ref[...] = carry_own[...].T.astype(F32)
 
     def drain():
         for copy in own_copies:
@@ -299,25 +328,19 @@
     sketch_pad = up(sketch, 128)
     chunk = up(-(-up(rank, 128) // size), 16)
     owners = -(-rank // chunk)
-    chunk_total = owners * chunk
-    rank_pad = up(chunk_total, 128)
-    owners = rank_pad // chunk if rank_pad % chunk == 0 else owners
     rank_pad = owners * chunk
-    core = jnp.pad(
-        train_cores[0].transpose(1, 0, 2), ((0, 0), (0, rank_pad - rank), (0, rank_pad - rank))
-    )
+    core = train_cores[0].transpose(1, 0, 2)
     gauss = jnp.pad(
         sketch_cores[0].transpose(1, 0, 2),
         ((0, 0), (0, sketch_pad - sketch), (0, sketch_pad - sketch)),
     )
-    left = jnp.pad(
-        left_interface.astype(BF16).T, ((0, rank_pad - rank), (0, sketch_pad - sketch))
-    )
-    right = jnp.pad(right_sketch, ((0, rank_pad - rank), (0, sketch_pad - sketch)))
+    sides = ((0, rank_pad - rank), (0, sketch_pad - sketch))
+    left = jnp.pad(left_interface.astype(BF16).T, sides)
+    right = jnp.pad(right_sketch, sides)
     scale = math.sqrt(sketch * modes * size)
     dims = (size, group_count, rank, sketch, modes, chunk, owners, scale)
     gram_rows = up(sketch, 8)
-    chunks = (owners, chunk, sketch_pad)
+    chunks = (rank_pad, sketch_pad)
     vmem = pl.BlockSpec(memory_space=pltpu.VMEM)
     dma = pltpu.SemaphoreType.DMA((size,))
     frames, faces = pl.pallas_call(
@@ -330,11 +353,11 @@
         out_specs=(vmem, vmem),
         scratch_shapes=[
             pltpu.VMEM(chunks, BF16),
-            pltpu.VMEM(chunks, F32),
-            pltpu.VMEM((size, chunk, sketch_pad), F32),
+            pltpu.VMEM((size * chunk, sketch_pad), BF16),
+            pltpu.VMEM((size, chunk, sketch_pad), BF16),
             pltpu.VMEM(chunks, BF16),
             pltpu.VMEM(chunks, BF16),
-            pltpu.VMEM(chunks, F32),
+            pltpu.VMEM((size * chunk, sketch_pad), F32),
             pltpu.VMEM((size, chunk, sketch_pad), F32),
             pltpu.VMEM((gram_rows, sketch_pad), F32),
             pltpu.VMEM((size, gram_rows, sketch_pad), F32),
@@ -342,7 +365,7 @@
             pltpu.VMEM((chunk, sketch_pad), BF16),
         ]
         + [dma] * 12,
-        compiler_params=pltpu.CompilerParams(has_side_effects=True),
+        compiler_params=pltpu.CompilerParams(collective_id=0, has_side_effects=True),
     )(core, gauss, left, right)
     frames = frames[:, :sketch, :sketch].transpose(1, 0, 2)[None]
     return frames, faces[None, :sketch, :rank]

time: 122 us -> 105 us (0.86)
  Pallas kernels: 112 us -> 93.1 us
  local copies, waits for them, and re-layouts: 8.81 us -> 10.2 us
    pallas_call x1, Pallas kernels: 112 us -> 93.1 us  [body(): pl.pallas_call(functools.partial(kernel, dims), out_shape=(jax.ShapeDtype...]
    unnamed x10 -> x4, local copies, waits for them, and re-layouts: 3.35 us -> 5.41 us
    pad x3 -> x2, local copies, waits for them, and re-layouts: 2.92 us -> 2.23 us  [the longest x1 1.56 us: body(): right = jnp.pad(right_sketch, sides)]
where the time goes in v2:
time: 105 us
  Pallas kernels  93.1 us (89%)
  local copies, waits for them, and re-layouts  10.2 us (10%)
    pallas_call x1, Pallas kernels, body(): pl.pallas_call(functools.partial(kernel, dims), out_shape=(jax.ShapeDtype...  93.1 us
    unnamed x4, local copies, waits for them, and re-layouts  5.41 us

profile of v2, /device:TPU:3, one launch (start us, length us, event | category | flops | bytes accessed | tf_op | source)
XLA Modules:
  0.0 104.9 jit_solution(4939358102469562123)
XLA Ops:
  0.6 0.9 convert_bitcast_fusion
  1.6 0.7 pad.12.left_ref
  2.2 0.9 copy.13
  3.2 0.7 pad.11.gauss_ref
  3.8 1.6 %pad.13.right_ref = bf16[448,128]{1,0:T(8,128)(2,1)} pad(bf16[400,100]{1,0:T(8,128)(2,1)} %param.7, bf16[]{:T(256)} %constant.2.clone.1), padding=0_48x0_28 | pad | bytes 194690 | tf_op jit(solution)/shard_map/jit(_pad)/pad | solution.py:339
  5.4 2.9 %copy.12 = bf16[1,400,4,400]{3,1,2,0:T(8,128)(2,1)} copy(bf16[1,400,4,400]{3,2,1,0:T(4,128)(2,1)} %param.4) | data formatting | bytes 2560000 | tf_op args[0]
  8.3 93.1 %shard_map.59 = (bf16[4,128,128]{2,1,0:T(8,128)(2,1)}, f32[128,448]{1,0:T(8,128)}) custom-call(bf16[4,400,400]{2,1,0:T(8,128)(2,1)} %bitcast.18, bf16[4,128,128]{2,1,0:T(8,128)(2,1)} %pad.11.gauss_ref, bf16[448,128]{1,0:T(8,128)(2,1)} %pad.12.left_ref, bf16[448,128]{1,0:T(8,128)(2,1)} %pad.13.right_ref), custom_call_target="tpu_custom_call" | custom-call | tf_op jit(solution)/shard_map/pallas_call | solution.py:346
  101.4 0.9 slice_bitcast_fusion.1
  102.4 0.7 copy.8
  103.0 0.9 slice_bitcast_fusion
  104.0 0.9 copy.9

commit v3 on v2

--- a/solution.py
+++ b/solution.py
@@ -183,13 +183,13 @@
         ).wait_recv()
 
     if rank_pad > rank:
-        rest = jnp.zeros((rank_pad - rank, sketch_pad), F32)
-        part_out[pl.ds(rank, rank_pad - rank), :] = rest.astype(part_out.dtype)
-        proj_out[pl.ds(rank, rank_pad - rank), :] = rest
+        proj_out[pl.ds(rank, rank_pad - rank), :] = jnp.zeros((rank_pad - rank, sketch_pad), F32)
+    part_out[...] = jnp.zeros(part_out.shape, part_out.dtype)
 
     @pl.when(group == final)
     def _():
-        sketch_buf[...] = right_ref[...]
+        sketch_buf[...] = jnp.zeros(sketch_buf.shape, BF16)
+        sketch_buf[pl.ds(0, rank), pl.ds(0, sketch)] = right_ref[...]
 
     @pl.when(group < final)
     def _():
@@ -205,9 +205,9 @@
     def _():
         total = None
         for i in range(modes):
-            term = dot(partials[i], gauss_ref[i], 1, 1)
+            term = dot(partials[i][:, :sketch], gauss_ref[i], 1, 1)
             total = term if total is None else total + term
-        part_out[pl.ds(0, rank), :] = total.astype(part_out.dtype)
+        part_out[pl.ds(0, rank), pl.ds(0, sketch)] = total.astype(part_out.dtype)
 
         @pl.when(group == final)
         def _():
@@ -231,7 +231,8 @@
 
     @pl.when(group == 0)
     def _():
-        carry_buf[...] = left_ref[...]
+        carry_buf[...] = jnp.zeros(carry_buf.shape, BF16)
+        carry_buf[pl.ds(0, rank), pl.ds(0, sketch)] = left_ref[...].T.astype(BF16)
 
     @pl.when(group > 0)
     def _():
@@ -249,8 +250,12 @@
     terms = dot(high, pair, 0, 0)
     cross = terms[:, sketch_pad:]
     gram = terms[:, :sketch_pad] + cross + cross.T
-    gram_rows = gram_out.shape[0]
-    gram_out[...] = gram[:gram_rows]
+    half, quarter = sketch_pad // 2, sketch_pad // 4
+    lower_rows = gram_out.shape[0] - quarter
+    gram_out[pl.ds(0, lower_rows), :] = gram[half : half + lower_rows]
+    gram_out[pl.ds(lower_rows, quarter), :] = jnp.concatenate(
+        [gram[:quarter, :half], gram[quarter:half, :half]], axis=1
+    )
     for copy in gram_copies:
         copy.start()
     built = jnp.concatenate(
@@ -267,8 +272,13 @@
     for source in range(size):
         term = gram_in[lax.rem(me - source + size, size)]
         total = term if total is None else total + term
-    if gram_rows < sketch_pad:
-        total = jnp.concatenate([total, jnp.zeros((sketch_pad - gram_rows, sketch_pad), F32)], 0)
+    lower = total[:lower_rows]
+    if lower_rows < half:
+        lower = jnp.concatenate([lower, jnp.zeros((half - lower_rows, sketch_pad), F32)], axis=0)
+    corner = total[lower_rows:]
+    corner = jnp.concatenate([corner[:, :half], corner[:, half:]], axis=0)
+    upper = jnp.concatenate([corner, lower.T[:half]], axis=1)
+    total = jnp.concatenate([upper, lower], axis=0)
     row_id = lax.broadcasted_iota(jnp.int32, (sketch_pad, sketch_pad), 0)
     lane_id = lax.broadcasted_iota(jnp.int32, (sketch_pad, sketch_pad), 1)
     total = jnp.where((row_id == lane_id) & (row_id >= sketch), 1.0, total)
@@ -330,16 +340,10 @@
     owners = -(-rank // chunk)
     rank_pad = owners * chunk
     core = train_cores[0].transpose(1, 0, 2)
-    gauss = jnp.pad(
-        sketch_cores[0].transpose(1, 0, 2),
-        ((0, 0), (0, sketch_pad - sketch), (0, sketch_pad - sketch)),
-    )
-    sides = ((0, rank_pad - rank), (0, sketch_pad - sketch))
-    left = jnp.pad(left_interface.astype(BF16).T, sides)
-    right = jnp.pad(right_sketch, sides)
+    gauss = sketch_cores[0].transpose(1, 0, 2)
     scale = math.sqrt(sketch * modes * size)
     dims = (size, group_count, rank, sketch, modes, chunk, owners, scale)
-    gram_rows = up(sketch, 8)
+    gram_rows = up(max(sketch - sketch_pad // 2, 8), 8) + sketch_pad // 4
     chunks = (rank_pad, sketch_pad)
     vmem = pl.BlockSpec(memory_space=pltpu.VMEM)
     dma = pltpu.SemaphoreType.DMA((size,))
@@ -366,7 +370,7 @@
         ]
         + [dma] * 12,
         compiler_params=pltpu.CompilerParams(collective_id=0, has_side_effects=True),
-    )(core, gauss, left, right)
+    )(core, gauss, left_interface, right_sketch)
     frames = frames[:, :sketch, :sketch].transpose(1, 0, 2)[None]
     return frames, faces[None, :sketch, :rank]
 

time: 105 us -> 99.7 us (0.950)
  Pallas kernels: 93.1 us -> 88.9 us
    pallas_call x1, Pallas kernels: 93.1 us -> 88.9 us  [body(): pl.pallas_call(functools.partial(kernel, dims), out_shape=(jax.ShapeDtype...]
    pad x3 -> x0, local copies, waits for them, and re-layouts: 2.91 us -> none  [the longest x1 1.56 us: body(): right = jnp.pad(right_sketch, sides)]
    unnamed x4 -> x5, local copies, waits for them, and re-layouts: 5.41 us -> 7.81 us
where the time goes in v3:
time: 99.7 us; the launch traced here: 99.3 us
  Pallas kernels  88.9 us (89%)
  local copies, waits for them, and re-layouts  9.67 us (10%)
    pallas_call x1, Pallas kernels, body(): pl.pallas_call(functools.partial(kernel, dims), out_shape=(jax.ShapeDtype...  88.9 us
    unnamed x5, local copies, waits for them, and re-layouts  7.81 us

profile of v3, /device:TPU:3, one launch (start us, length us, event | category | flops | bytes accessed | tf_op | source)
XLA Modules:
  0.0 99.3 jit_solution(15290957008818411397)
XLA Ops:
  0.6 1.6 %copy.14 = bf16[1,100,4,100]{3,1,2,0:T(8,128)(2,1)} copy(bf16[1,100,4,100]{3,2,1,0:T(4,128)(2,1)} %param.5) | data formatting | bytes 160000 | tf_op args[1]
  2.2 1.8 %copy.8.left_ref = f32[100,400]{1,0:T(8,128)} copy(f32[100,400]{0,1:T(8,128)} %param.6) | data formatting | bytes 320000 | tf_op args[2]
  3.9 2.9 %copy.13 = bf16[1,400,4,400]{3,1,2,0:T(8,128)(2,1)} copy(bf16[1,400,4,400]{3,2,1,0:T(4,128)(2,1)} %param.4) | data formatting | bytes 2560000 | tf_op args[0]
  6.9 88.9 %shard_map.59 = (bf16[4,128,128]{2,1,0:T(8,128)(2,1)}, f32[128,448]{1,0:T(8,128)}) custom-call(bf16[4,400,400]{2,1,0:T(8,128)(2,1)} %bitcast.16, bf16[4,100,100]{2,1,0:T(8,128)(2,1)} %bitcast.17, f32[100,400]{1,0:T(8,128)} %copy.8.left_ref, bf16[400,100]{1,0:T(8,128)(2,1)} %right_ref.1), custom_call_target="tpu_custom_call" | custom-call | tf_op jit(solution)/shard_map/pallas_call | solution.py:350
  95.8 0.9 slice_bitcast_fusion.1
  96.7 0.7 copy.9
  97.4 0.9 slice_bitcast_fusion
  98.4 0.9 copy.10
